TPU v7x, 32 devices: a whole 2x2x4 slice. The times are simulated.
32 devices in a mesh: dp: 16 (over z, y, core), tensor: 2 (over x).
Axes of the slice: x: 2, y: 2, z: 4, core: 2. Of those that a mesh axis runs over, the one named last changes fastest.
Arguments:
- training_token_input: bfloat16 [4096, 8192], P('dp', 'tensor'), may hold values from -6 to 6
- gate_output_gradient: bfloat16 [4096, 29568], P('dp', 'tensor'), may hold values from -6 to 6
- up_output_gradient: bfloat16 [4096, 29568], P('dp', 'tensor'), may hold values from -6 to 6
- gate_first_matrix: bfloat16 [8192, 64], P('tensor'), may hold values from -0.0625 to 0.0625
- gate_second_matrix: bfloat16 [64, 29568], P(None, 'tensor'), may hold values from -0.75 to 0.75
- up_first_matrix: bfloat16 [8192, 64], P('tensor'), may hold values from -0.0625 to 0.0625
- up_second_matrix: bfloat16 [64, 29568], P(None, 'tensor'), may hold values from -0.75 to 0.75
- gate_weight_base: bfloat16 [8192, 29568], P('tensor', 'dp'), may hold values from -0.0625 to 0.0625
- up_weight_base: bfloat16 [8192, 29568], P('tensor', 'dp'), may hold values from -0.0625 to 0.0625
- down_weight_base: bfloat16 [29568, 8192], P('dp', 'tensor'), may hold values from -0.03125 to 0.03125
- decode_step_input: bfloat16 [2, 512, 8192], P(None, None, 'tensor'), may hold values from -6 to 6
Outputs:
- decoded: bfloat16 [2, 512, 8192], P(None, None, 'tensor')
All inputs are finite; a program needn't handle non-finite values.
Results may differ from a plain program's by a relative error of at most 0.04.
Values may be sent and summed in bfloat16 or wider, within the bound.
A program may use at most 192 MiB of HBM per device.

v0:
```python
import math

import jax
import jax.numpy as jnp
from jax import lax
from jax.sharding import PartitionSpec as P

MODEL_WIDTH = 8192
HIDDEN_UNITS = 29568
ADAPTER_RANK = 64


def from_root(value, axis, source):
    kept = jnp.where(lax.axis_index(axis) == source, value, 0).astype(value.dtype)
    return lax.psum(kept, axis)


def on_device(
    training_token_input,
    gate_output_gradient,
    up_output_gradient,
    gate_first_matrix,
    gate_second_matrix,
    up_first_matrix,
    up_second_matrix,
    gate_weight_base,
    up_weight_base,
    down_weight_base,
    decode_step_input,
):
    single_float = jnp.float32
    brain_float_half = jnp.bfloat16
    tokens_total = training_token_input.shape[0] * lax.axis_size("dp")
    second_learning_rate = 0.5 / math.sqrt(ADAPTER_RANK * tokens_total)
    first_learning_rate = 0.5 / math.sqrt(MODEL_WIDTH * HIDDEN_UNITS * tokens_total / ADAPTER_RANK)
    partials = (
        jnp.dot(training_token_input, gate_first_matrix, preferred_element_type=single_float),
        jnp.dot(training_token_input, up_first_matrix, preferred_element_type=single_float),
        jnp.dot(gate_output_gradient, gate_second_matrix.T, preferred_element_type=single_float),
        jnp.dot(up_output_gradient, up_second_matrix.T, preferred_element_type=single_float),
    )
    summed = (
        lax.psum(partials[0].astype(jnp.bfloat16), "tensor").astype(jnp.float32),
        lax.psum(partials[1].astype(jnp.bfloat16), "tensor").astype(jnp.float32),
        lax.psum(partials[2].astype(jnp.bfloat16), "tensor").astype(jnp.float32),
        lax.psum(partials[3].astype(jnp.bfloat16), "tensor").astype(jnp.float32),
    )
    inner_bg, inner_bu, inner_ag, inner_au = [piece.astype(brain_float_half) for piece in summed]
    gate_second_gradient = jnp.dot(
        inner_bg.T, gate_output_gradient, preferred_element_type=single_float
    )
    up_second_gradient = jnp.dot(
        inner_bu.T, up_output_gradient, preferred_element_type=single_float
    )
    gate_first_gradient = jnp.dot(
        training_token_input.T, inner_ag, preferred_element_type=single_float
    )
    up_first_gradient = jnp.dot(
        training_token_input.T, inner_au, preferred_element_type=single_float
    )
    gate_second_gradient, up_second_gradient, gate_first_gradient, up_first_gradient = (
        lax.psum(gate_second_gradient.astype(jnp.bfloat16), "dp").astype(jnp.float32),
        lax.psum(up_second_gradient.astype(jnp.bfloat16), "dp").astype(jnp.float32),
        lax.psum(gate_first_gradient.astype(jnp.bfloat16), "dp").astype(jnp.float32),
        lax.psum(up_first_gradient.astype(jnp.bfloat16), "dp").astype(jnp.float32),
    )
    stepped_gate_second = (
        gate_second_matrix.astype(single_float) - second_learning_rate * gate_second_gradient
    ).astype(brain_float_half)
    stepped_up_second = (
        up_second_matrix.astype(single_float) - second_learning_rate * up_second_gradient
    ).astype(brain_float_half)
    stepped_gate_first = (
        gate_first_matrix.astype(single_float) - first_learning_rate * gate_first_gradient
    ).astype(brain_float_half)
    stepped_up_first = (
        up_first_matrix.astype(single_float) - first_learning_rate * up_first_gradient
    ).astype(brain_float_half)
    group = lax.axis_size("dp") // lax.axis_size("tensor")
    replica = lax.axis_index("dp")
    source = replica // group
    columns = gate_weight_base.shape[1]
    offset = replica % group * columns
    cols_gate = lax.dynamic_slice_in_dim(stepped_gate_second, offset, columns, 1)
    cols_up = lax.dynamic_slice_in_dim(stepped_up_second, offset, columns, 1)
    cols_gate, cols_up = (
        from_root(cols_gate, "tensor", source),
        from_root(cols_up, "tensor", source),
    )
    combined_gate_weight = (
        gate_weight_base.astype(single_float)
        + jnp.dot(stepped_gate_first, cols_gate, preferred_element_type=single_float)
    ).astype(brain_float_half)
    combined_up_weight = (
        up_weight_base.astype(single_float)
        + jnp.dot(stepped_up_first, cols_up, preferred_element_type=single_float)
    ).astype(brain_float_half)
    results = []
    for position in range(decode_step_input.shape[0]):
        rows_in = decode_step_input[position]
        gate_part = jnp.dot(rows_in, combined_gate_weight, preferred_element_type=single_float)
        up_part = jnp.dot(rows_in, combined_up_weight, preferred_element_type=single_float)
        gate, upper = (
            lax.psum_scatter(
                gate_part.astype(jnp.bfloat16), "tensor", scatter_dimension=0, tiled=True
            ).astype(jnp.float32),
            lax.psum_scatter(
                up_part.astype(jnp.bfloat16), "tensor", scatter_dimension=0, tiled=True
            ).astype(jnp.float32),
        )
        local_hidden = (jax.nn.silu(gate) * upper).astype(brain_float_half)
        hidden = lax.all_gather(local_hidden, "tensor", axis=0, tiled=True)
        out_part = jnp.dot(hidden, down_weight_base, preferred_element_type=single_float)
        results.append(
            lax.psum(out_part.astype(jnp.bfloat16), "dp")
            .astype(jnp.float32)
            .astype(brain_float_half)
        )
    return jnp.stack(results)


def solution(mesh):
    placed = (
        P("dp", "tensor"),
        P("dp", "tensor"),
        P("dp", "tensor"),
        P("tensor", None),
        P(None, "tensor"),
        P("tensor", None),
        P(None, "tensor"),
        P("tensor", "dp"),
        P("tensor", "dp"),
        P("dp", "tensor"),
        P(None, None, "tensor"),
    )
    return jax.shard_map(
        on_device, mesh=mesh, in_specs=placed, out_specs=P(None, None, "tensor"), check_vma=False
    )
```

profile of v0, /device:TPU:0, one launch (start us, length us, event | category | flops | bytes accessed | tf_op | source)
XLA Modules:
  0.0 632.4 jit_solution(14241953879334761086)
XLA Ops:
  6.5 1.6 copy-done
  8.1 2.5 convolution_convert_fusion.8
  10.6 2.4 convolution_convert_fusion.6
  13.0 6.6 %convolution_convert_fusion.9 = bf16[256,64]{1,0:T(8,128)(2,1)} fusion(bf16[256,14784]{0,1:T(8,128)(2,1)} %param.12, bf16[64,14784]{1,0:T(8,128)(2,1)} %param.15), kind=kOutput, calls=%fused_computation.50 | convolution fusion | flops 484458496 | bytes 9494528 | tf_op jit(solution)/shard_map/dot_general | solution.py:39
  19.7 2.8 convolution_convert_fusion.7
  22.6 26.3 %all-reduce.13.cloned.1.call-done = (bf16[256,64]{1,0:T(8,128)(2,1)}, bf16[256,64]{1,0:T(8,128)(2,1)}, bf16[256,64]{1,0:T(8,128)(2,1)}, bf16[256,64]{1,0:T(8,128)(2,1)}) async-done(((bf16[256,64]{1,0:T(8,128)(2,1)}, bf16[256,64]{1,0:T(8,128)(2,1)}, bf16[256,64]{1,0:T(8,128)(2,1)}, bf16[256,64]{1,0:T(8,128)(2,1)}), (bf16[256,64]{1,0:T(8,128)(2,1)}, bf16[256,64]{1,0:T(8,128)(2,1)}, bf16[256,64]{1,0:T(8,128)(2,1)}, ...) | async-done | bytes 131088 | tf_op jit(solution)/shard_map/psum | solution.py:44
  48.9 2.2 fusion.3
  51.1 2.3 fusion.2
  53.4 6.9 %convolution_convert_fusion = bf16[64,14784]{1,0:T(8,128)(2,1)} fusion(bf16[256,64]{1,0:T(8,128)(2,1)S(1)} %copy-done.7, bf16[256,14784]{0,1:T(8,128)(2,1)} %param.13), kind=kOutput, calls=%fused_computation.2 | convolution fusion | flops 485388288 | bytes 9494528 | tf_op jit(solution)/shard_map/dot_general | solution.py:52
  60.3 3.7 convolution_convert_fusion.1
  64.1 119.4 %all-reduce.11.cloned.1.call-done = (bf16[64,14784]{1,0:T(8,128)(2,1)}, bf16[4096,64]{0,1:T(8,128)(2,1)}, bf16[64,14784]{1,0:T(8,128)(2,1)}, bf16[4096,64]{0,1:T(8,128)(2,1)}) async-done(((bf16[64,14784]{1,0:T(8,128)(2,1)}, bf16[4096,64]{0,1:T(8,128)(2,1)}, bf16[64,14784]{1,0:T(8,128)(2,1)}, bf16[4096,64]{0,1:T(8,128)(2,1)}), (bf16[64,14784]{1,0:T(8,128)(2,1)}, bf16[4096,64]{0,1:T(8,128)(2,1)}, ...) | async-done | bytes 4833296 | tf_op jit(solution)/shard_map/psum | solution.py:63
  183.5 2.5 fusion.52
  186.3 27.7 %all-reduce.15.cloned.1.call-done = (bf16[64,1848]{1,0:T(8,128)(2,1)}, bf16[64,1848]{1,0:T(8,128)(2,1)}) async-done(((bf16[64,1848]{1,0:T(8,128)(2,1)}, bf16[64,1848]{1,0:T(8,128)(2,1)}), (bf16[64,1848]{1,0:T(8,128)(2,1)}, bf16[64,1848]{1,0:T(8,128)(2,1)})) %all-reduce.15.cloned.1.call-update) | async-done | bytes 473104 | tf_op jit(solution)/shard_map/psum | solution.py:15
  214.0 15.1 %add_convert_fusion = bf16[4096,1848]{0,1:T(8,128)(2,1)} fusion(bf16[4096,1848]{0,1:T(8,128)(2,1)} %param.19, bf16[64,1848]{1,0:T(8,128)(2,1)} %get-tuple-element.15, bf16[4096,64]{0,1:T(8,128)(2,1)} %get-tuple-element.8, bf16[4096,64]{0,1:T(8,128)(2,1)S(1)} %copy-done.2), kind=kOutput, calls=%fused_computation | convolution fusion | flops 992903168 | bytes 31562752 | tf_op jit(solution)/shard_map/dot_general | solution.py:96
  229.0 13.6 %fusion.28 = bf16[512,1848]{0,1:T(8,128)(2,1)} fusion(bf16[4096,1848]{0,1:T(8,128)(2,1)} %add_convert_fusion, bf16[2,512,4096]{2,1,0:T(8,128)(2,1)} %param.21), kind=kOutput, calls=%fused_computation.29 | convolution fusion | flops 7752019968 | bytes 21225472 | tf_op jit(solution)/shard_map/dot_general | solution.py:102
  242.7 0.3 reduce-scatter.9.cloned.1.call-start
  243.0 10.7 %add_convert_fusion.1 = bf16[4096,1848]{0,1:T(8,128)(2,1)} fusion(bf16[4096,1848]{0,1:T(8,128)(2,1)} %param.18, bf16[64,1848]{1,0:T(8,128)(2,1)S(1)} %copy-done.5, bf16[4096,64]{0,1:T(8,128)(2,1)S(1)} %copy-done.4, bf16[4096,64]{0,1:T(8,128)(2,1)S(1)} %copy-done.3), kind=kOutput, calls=%fused_computation.1 | convolution fusion | flops 992903168 | bytes 31562752 | tf_op jit(solution)/shard_map/dot_general | solution.py:92
  253.7 13.6 %fusion.31 = bf16[512,1848]{0,1:T(8,128)(2,1)} fusion(bf16[4096,1848]{0,1:T(8,128)(2,1)} %add_convert_fusion.1, bf16[2,512,4096]{2,1,0:T(8,128)(2,1)} %param.21), kind=kOutput, calls=%fused_computation.30 | convolution fusion | flops 7752019968 | bytes 21225472 | tf_op jit(solution)/shard_map/dot_general | solution.py:101
  267.3 13.6 %fusion.34 = bf16[512,1848]{0,1:T(8,128)(2,1)} fusion(bf16[4096,1848]{0,1:T(8,128)(2,1)} %add_convert_fusion, bf16[2,512,4096]{2,1,0:T(8,128)(2,1)} %param.21), kind=kOutput, calls=%fused_computation.31 | convolution fusion | flops 7752019968 | bytes 21225472 | tf_op jit(solution)/shard_map/dot_general | solution.py:102
  280.9 0.3 reduce-scatter.5.cloned.1.call-start
  281.2 13.6 %fusion.37 = bf16[512,1848]{0,1:T(8,128)(2,1)} fusion(bf16[4096,1848]{0,1:T(8,128)(2,1)} %add_convert_fusion.1, bf16[2,512,4096]{2,1,0:T(8,128)(2,1)} %param.21), kind=kOutput, calls=%fused_computation.32 | convolution fusion | flops 7752019968 | bytes 21225472 | tf_op jit(solution)/shard_map/dot_general | solution.py:101
  294.9 9.4 %reduce-scatter.9.cloned.1.call-done = bf16[256,1848]{0,1:T(8,128)(2,1)} async-done(((bf16[512,1848]{0,1:T(8,128)(2,1)}), bf16[256,1848]{0,1:T(8,128)(2,1)}) %reduce-scatter.9.cloned.1.call-update) | async-done | bytes 946192 | tf_op jit(solution)/shard_map/reduce_scatter | solution.py:104
  304.3 3.0 fusion.48
  307.4 28.8 %reduce-scatter.7.cloned.1.call-done = bf16[256,1848]{0,1:T(8,128)(2,1)} async-done(((bf16[512,1848]{0,1:T(8,128)(2,1)}), bf16[256,1848]{0,1:T(8,128)(2,1)}) %reduce-scatter.7.cloned.1.call-update) | async-done | bytes 946192 | tf_op jit(solution)/shard_map/reduce_scatter | solution.py:107
  336.1 32.0 %reduce-scatter.5.cloned.1.call-done = bf16[256,1848]{0,1:T(8,128)(2,1)} async-done(((bf16[512,1848]{0,1:T(8,128)(2,1)}), bf16[256,1848]{0,1:T(8,128)(2,1)}) %reduce-scatter.5.cloned.1.call-update) | async-done | bytes 946192 | tf_op jit(solution)/shard_map/reduce_scatter | solution.py:104
  368.1 3.0 fusion.49
  371.2 29.2 %all-gather.5.cloned.1.call-done = bf16[512,1848]{0,1:T(8,128)(2,1)} async-done(((bf16[256,1848]{0,1:T(8,128)(2,1)}), bf16[512,1848]{0,1:T(8,128)(2,1)}) %all-gather.5.cloned.1.call-update) | async-done | bytes 1892368 | tf_op jit(solution)/shard_map/all_gather | solution.py:112
  400.4 14.2 %fusion.1 = bf16[1,512,4096]{2,1,0:T(8,128)(2,1)} fusion(bf16[512,1848]{0,1:T(8,128)(2,1)} %all-gather.5.cloned.1.call-done, bf16[1848,4096]{1,0:T(8,128)(2,1)} %param.20), kind=kOutput, calls=%fused_computation.8 | convolution fusion | flops 7753170944 | bytes 21225472 | tf_op jit(solution)/shard_map/dot_general | solution.py:113
  414.6 18.1 %all-gather.3.cloned.1.call-done = bf16[512,1848]{0,1:T(8,128)(2,1)} async-done(((bf16[256,1848]{0,1:T(8,128)(2,1)}), bf16[512,1848]{0,1:T(8,128)(2,1)}) %all-gather.3.cloned.1.call-update) | async-done | bytes 1892368 | tf_op jit(solution)/shard_map/all_gather | solution.py:112
  432.7 14.3 %fusion = bf16[1,512,4096]{2,1,0:T(8,128)(2,1)} fusion(bf16[512,1848]{0,1:T(8,128)(2,1)} %all-gather.3.cloned.1.call-done, bf16[1848,4096]{1,0:T(8,128)(2,1)} %param.20), kind=kOutput, calls=%fused_computation.7 | convolution fusion | flops 7753170944 | bytes 21225472 | tf_op jit(solution)/shard_map/dot_general | solution.py:113
  447.1 170.3 %all-reduce.9.cloned.1.call-done = (bf16[1,512,4096]{2,1,0:T(8,128)(2,1)}, bf16[1,512,4096]{2,1,0:T(8,128)(2,1)}) async-done(((bf16[1,512,4096]{2,1,0:T(8,128)(2,1)}, bf16[1,512,4096]{2,1,0:T(8,128)(2,1)}), (bf16[1,512,4096]{2,1,0:T(8,128)(2,1)}, bf16[1,512,4096]{2,1,0:T(8,128)(2,1)})) %all-reduce.9.cloned.1.call-update) | async-done | bytes 8388624 | tf_op jit(solution)/shard_map/psum | solution.py:115
  617.4 7.8 %pad_maximum_fusion = bf16[2,512,4096]{2,1,0:T(8,128)(2,1)} fusion(bf16[1,512,4096]{2,1,0:T(8,128)(2,1)} %get-tuple-element.5, bf16[1,512,4096]{2,1,0:T(8,128)(2,1)} %get-tuple-element.6), kind=kLoop, calls=%fused_computation.4 | loop fusion | flops 4194304 | bytes 16777216 | tf_op jit(solution)/shard_map/stack | solution.py:119
  (46 shorter events, 0.7 us)
Async XLA Ops:
  6.5 1.6 copy-start
  6.5 42.3 %all-reduce.13.cloned.1.call-start = ((), (), s32[]{:S(2)}) async-start(), calls=%async_computation.12 | async-start | bytes 524288 | tf_op jit(solution)/shard_map/psum | solution.py:44
  8.1 11.5 %slice-start = ((s8[7569408]{0:T(1024)(128)(4,1)}), s8[4194304]{0:T(1024)(128)(4,1)S(1)}, s32[]{:S(2)}) async-start(s8[7569408]{0:T(1024)(128)(4,1)} %bitcast.68), calls=%async_computation.14 | async-start | bytes 8388608
  13.0 6.7 %slice-start.1 = ((s8[7569408]{0:T(1024)(128)(4,1)}), s8[3375104]{0:T(1024)(128)(4,1)S(1)}, s32[]{:S(2)}) async-start(s8[7569408]{0:T(1024)(128)(4,1)} %bitcast.68), calls=%async_computation.15 | async-start | bytes 6750208
  13.0 6.7 %copy-start.8 = (bf16[64,14784]{1,0:T(8,128)(2,1)S(1)}, bf16[64,14784]{1,0:T(8,128)(2,1)}, u32[]{:S(2)}) copy-start(bf16[64,14784]{1,0:T(8,128)(2,1)} %param.17) | copy-start | bytes 5677060
  22.5 161.0 %all-reduce.11.cloned.1.call-start = ((), (), s32[]{:S(2)}) async-start(), calls=%async_computation.11 | async-start | bytes 9699328 | tf_op jit(solution)/shard_map/psum | solution.py:63
  48.9 4.5 copy-start.7
  51.1 9.3 %slice-start.2 = ((s8[7569408]{0:T(1024)(128)(4,1)}), s8[4194304]{0:T(1024)(128)(4,1)S(1)}, s32[]{:S(2)}) async-start(s8[7569408]{0:T(1024)(128)(4,1)} %bitcast.70), calls=%async_computation.16 | async-start | bytes 8388608
  53.4 7.0 %slice-start.3 = ((s8[7569408]{0:T(1024)(128)(4,1)}), s8[3375104]{0:T(1024)(128)(4,1)S(1)}, s32[]{:S(2)}) async-start(s8[7569408]{0:T(1024)(128)(4,1)} %bitcast.70), calls=%async_computation.17 | async-start | bytes 6750208
  53.4 7.0 %copy-start.6 = (bf16[256,64]{1,0:T(8,128)(2,1)S(1)}, bf16[256,64]{1,0:T(8,128)(2,1)}, u32[]{:S(2)}) copy-start(bf16[256,64]{1,0:T(8,128)(2,1)} %get-tuple-element.13) | copy-start | bytes 98308
  64.0 149.9 %copy-start.2 = (bf16[4096,64]{0,1:T(8,128)(2,1)S(1)}, bf16[4096,64]{0,1:T(8,128)(2,1)}, u32[]{:S(2)}) copy-start(bf16[4096,64]{0,1:T(8,128)(2,1)} %param.16) | copy-start | bytes 1572868
  64.1 149.9 %all-reduce.15.cloned.1.call-start = ((), (), s32[]{:S(2)}) async-start(), calls=%async_computation.13 | async-start | bytes 983040 | tf_op jit(solution)/shard_map/psum | solution.py:15
  186.0 108.8 %reduce-scatter.11.cloned.1.call-start = ((), (), s32[]{:S(2)}) async-start(), calls=%async_computation.8 | async-start | bytes 2838528 | tf_op jit(solution)/shard_map/reduce_scatter | solution.py:107
  229.0 13.9 %copy-start.3 = (bf16[4096,64]{0,1:T(8,128)(2,1)S(1)}, bf16[4096,64]{0,1:T(8,128)(2,1)}, u32[]{:S(2)}) copy-start(bf16[4096,64]{0,1:T(8,128)(2,1)} %param.14) | copy-start | bytes 1572868
  229.0 13.9 %copy-start.4 = (bf16[4096,64]{0,1:T(8,128)(2,1)S(1)}, bf16[4096,64]{0,1:T(8,128)(2,1)}, u32[]{:S(2)}) copy-start(bf16[4096,64]{0,1:T(8,128)(2,1)} %get-tuple-element.10) | copy-start | bytes 1572868
  229.0 13.9 %copy-start.5 = (bf16[64,1848]{1,0:T(8,128)(2,1)S(1)}, bf16[64,1848]{1,0:T(8,128)(2,1)}, u32[]{:S(2)}) copy-start(bf16[64,1848]{1,0:T(8,128)(2,1)} %get-tuple-element.16) | copy-start | bytes 709636
  242.7 61.6 %reduce-scatter.9.cloned.1.call-start = ((), (), s32[]{:S(2)}) async-start(), calls=%async_computation.7 | async-start | bytes 2838528 | tf_op jit(solution)/shard_map/reduce_scatter | solution.py:104
  267.3 68.9 %reduce-scatter.7.cloned.1.call-start = ((), (), s32[]{:S(2)}) async-start(), calls=%async_computation.5 | async-start | bytes 2838528 | tf_op jit(solution)/shard_map/reduce_scatter | solution.py:107
  280.9 87.2 %reduce-scatter.5.cloned.1.call-start = ((), (), s32[]{:S(2)}) async-start(), calls=%async_computation.4 | async-start | bytes 2838528 | tf_op jit(solution)/shard_map/reduce_scatter | solution.py:104
  294.8 105.6 %all-gather.5.cloned.1.call-start = ((), (), s32[]{:S(2)}) async-start(), calls=%async_computation.9 | async-start | bytes 2838528 | tf_op jit(solution)/shard_map/all_gather | solution.py:112
  307.3 125.4 %all-gather.3.cloned.1.call-start = ((), (), s32[]{:S(2)}) async-start(), calls=%async_computation.6 | async-start | bytes 2838528 | tf_op jit(solution)/shard_map/all_gather | solution.py:112
  371.1 246.2 %all-reduce.9.cloned.1.call-start = ((), (), s32[]{:S(2)}) async-start(), calls=%async_computation.10 | async-start | bytes 16777216 | tf_op jit(solution)/shard_map/psum | solution.py:115
  617.4 7.8 %copy-start.1 = (bf16[256,4096]{1,0:T(8,128)(2,1)S(1)}, bf16[256,4096]{1,0:T(8,128)(2,1)}, u32[]{:S(2)}) copy-start(bf16[256,4096]{1,0:T(8,128)(2,1)} %param.11) | copy-start | bytes 6291460
Sparse Core Ops, SparseCore 0:
  22.6 26.1 all-reduce.12
  64.2 119.3 all-reduce.10
  186.2 27.7 all-reduce.14
  242.8 29.6 reduce-scatter.10
  274.6 29.6 reduce-scatter.8
  306.4 29.6 reduce-scatter.6
  338.4 29.6 reduce-scatter.4
  369.6 30.7 all-gather.4
  401.9 30.7 all-gather.2
  447.2 170.1 all-reduce.8
where the time goes:
time: 640 us; the launch traced here: 632 us
  waiting for transfers between devices  461 us (72%)
  matrix products  138 us (22%)
  other arithmetic  16.2 us (3%)
  between operations  14.1 us (2%)
    psum x1, waiting for transfers between devices, on_device(): lax.psum(out_part.astype(jnp.bfloat16), 'dp').astype(jnp.float32)  170 us
    psum x1, waiting for transfers between devices, on_device(): lax.psum(up_second_gradient.astype(jnp.bfloat16), 'dp').astype(jnp.float32)  119 us
    all_gather x2, waiting for transfers between devices, on_device(): hidden = lax.all_gather(local_hidden, 'tensor', axis=0, tiled=True)  47.4 us
    reduce_scatter x2, waiting for transfers between devices, on_device(): lax.psum_scatter(gate_part.astype(jnp.bfloat16), 'tensor', scatter_dimens...  41.4 us
    reduce_scatter x2, waiting for transfers between devices, on_device(): lax.psum_scatter(up_part.astype(jnp.bfloat16), 'tensor', scatter_dimensio...  28.8 us
    dot_general x2, matrix products, on_device(): jnp.dot(hidden, down_weight_base, preferred_element_type=single_float)  28.5 us
    psum x1, waiting for transfers between devices, from_root(): return lax.psum(kept, axis)  27.7 us
    dot_general x2, matrix products, on_device(): jnp.dot(rows_in, combined_up_weight, preferred_element_type=single_float)  27.2 us
  transfers between devices with their start and end apart: 10, of which 9 were waited for; matrix products, arithmetic and copies ran while one was open for 11% of the time, Pallas kernels for 0%

commit v1 on v0

v1 whole, which is shorter than its diff:
```python
import math

import jax
import jax.numpy as jnp
from jax import lax
from jax.sharding import PartitionSpec as P

MODEL_WIDTH = 8192
HIDDEN_UNITS = 29568
ADAPTER_RANK = 64


def swap(value):
    return lax.ppermute(value, "tensor", ((0, 1), (1, 0)))


def pair_sum(value):
    if lax.axis_size("tensor") == 2:
        sent = value.astype(jnp.bfloat16)
        return sent.astype(jnp.float32) + swap(sent).astype(jnp.float32)
    return lax.psum(value.astype(jnp.bfloat16), "tensor").astype(jnp.float32)


def row_share(value, index):
    rows = value.shape[1] // lax.axis_size("tensor")
    return lax.dynamic_slice_in_dim(value, index * rows, rows, 1)


def on_device(
    training_token_input,
    gate_output_gradient,
    up_output_gradient,
    gate_first_matrix,
    gate_second_matrix,
    up_first_matrix,
    up_second_matrix,
    gate_weight_base,
    up_weight_base,
    down_weight_base,
    decode_step_input,
):
    f32, bf16 = jnp.float32, jnp.bfloat16
    n_dp, n_tensor = lax.axis_size("dp"), lax.axis_size("tensor")
    me = lax.axis_index("tensor")
    replica = lax.axis_index("dp")
    rank = gate_first_matrix.shape[1]
    tokens_total = training_token_input.shape[0] * n_dp
    second_learning_rate = 0.5 / math.sqrt(ADAPTER_RANK * tokens_total)
    first_learning_rate = 0.5 / math.sqrt(MODEL_WIDTH * HIDDEN_UNITS * tokens_total / ADAPTER_RANK)

    def dot(left, right, over):
        return lax.dot_general(left, right, (over, ((), ())), preferred_element_type=f32)

    firsts = jnp.concatenate([gate_first_matrix, up_first_matrix], axis=1)
    inner = jnp.concatenate(
        [
            jnp.dot(training_token_input, firsts, preferred_element_type=f32),
            dot(gate_output_gradient, gate_second_matrix, ((1,), (1,))),
            dot(up_output_gradient, up_second_matrix, ((1,), (1,))),
        ],
        axis=1,
    )
    inner = pair_sum(inner).astype(bf16)
    inner_b, inner_a = inner[:, : 2 * rank], inner[:, 2 * rank :]

    columns = gate_weight_base.shape[1]
    group = n_dp // n_tensor
    unit = 16 * n_tensor
    padded = -(-columns // unit) * unit
    piece = padded // n_tensor
    second_gradient = jnp.concatenate(
        [
            dot(gate_output_gradient, inner_b[:, :rank], ((0,), (0,))).astype(bf16),
            dot(up_output_gradient, inner_b[:, rank:], ((0,), (0,))).astype(bf16),
        ],
        axis=1,
    )
    second_gradient = jnp.pad(
        second_gradient.reshape(group, columns, 2 * rank),
        ((0, 0), (0, padded - columns), (0, 0)),
    ).reshape(group * padded, 2 * rank)
    first_gradient = dot(training_token_input, inner_a, ((0,), (0,))).astype(bf16)

    rows_in, second_gradient, first_gradient = lax.optimization_barrier(
        (decode_step_input, second_gradient, first_gradient)
    )
    second_gradient = lax.psum_scatter(second_gradient, "dp", scatter_dimension=0, tiled=True)
    first_gradient = lax.psum(first_gradient, "dp")

    def base(rows, weight):
        return dot(rows, weight, ((2,), (0,))).astype(bf16)

    weights = (gate_weight_base, up_weight_base)
    if n_tensor == 2:
        theirs = row_share(rows_in, 1 - me)
        ours = row_share(rows_in, me)
        arrived = [swap(base(theirs, weight)) for weight in weights]
        base_sums = [
            base(ours, weight).astype(f32) + other.astype(f32)
            for weight, other in zip(weights, arrived)
        ]
    else:
        base_sums = [
            lax.psum_scatter(
                base(rows_in, weight), "tensor", scatter_dimension=1, tiled=True
            ).astype(f32)
            for weight in weights
        ]

    start = replica // n_tensor * columns + replica % n_tensor * piece

    def old_piece(matrix):
        wide = jnp.pad(matrix, ((0, 0), (0, padded)))
        return lax.dynamic_slice_in_dim(wide, start, piece, 1).T

    old = jnp.concatenate([old_piece(gate_second_matrix), old_piece(up_second_matrix)], axis=1)
    stepped = (
        old.astype(f32) - second_learning_rate * second_gradient.astype(f32)
    ).astype(bf16)
    routes = [
        (
            (block * n_tensor + part) * n_tensor + side,
            (side * group + block) * n_tensor + part,
        )
        for block in range(group)
        for part in range(n_tensor)
        for side in range(n_tensor)
    ]
    stepped = lax.ppermute(stepped, ("dp", "tensor"), routes)
    if n_tensor == 2:
        other = swap(stepped)
        first_half = me == 0
        seconds = jnp.concatenate(
            [jnp.where(first_half, stepped, other), jnp.where(first_half, other, stepped)], axis=0
        )
    else:
        seconds = lax.all_gather(stepped, "tensor", axis=0, tiled=True)
    seconds = seconds[:columns]

    new_firsts = (
        firsts.astype(f32) - first_learning_rate * first_gradient.astype(f32)
    ).astype(bf16)
    low = dot(rows_in, new_firsts, ((2,), (0,)))
    if n_tensor == 2:
        low = row_share(low, me) + swap(row_share(low, 1 - me).astype(bf16)).astype(f32)
    else:
        low = lax.psum_scatter(
            low.astype(bf16), "tensor", scatter_dimension=1, tiled=True
        ).astype(f32)
    low = low.astype(bf16)

    gate = base_sums[0] + dot(low[..., :rank], seconds[:, :rank], ((2,), (1,)))
    upper = base_sums[1] + dot(low[..., rank:], seconds[:, rank:], ((2,), (1,)))
    hidden = (jax.nn.silu(gate) * upper).astype(bf16)

    def project(part):
        steps, rows, _ = part.shape
        out = dot(part, down_weight_base, ((2,), (0,))).astype(bf16)
        out = out.reshape(steps * rows, -1)
        out = lax.psum_scatter(out, "dp", scatter_dimension=0, tiled=True)
        out = lax.all_gather(out, "dp", axis=0, tiled=True)
        return out.reshape(steps, rows, -1)

    if n_tensor == 2:
        own = project(hidden)
        other = project(swap(hidden))
        share = hidden.shape[1]
        result = jnp.zeros(decode_step_input.shape[:2] + (own.shape[2],), bf16)
        result = lax.dynamic_update_slice_in_dim(result, own, me * share, 1)
        return lax.dynamic_update_slice_in_dim(result, other, (1 - me) * share, 1)
    return project(lax.all_gather(hidden, "tensor", axis=1, tiled=True))


def solution(mesh):
    placed = (
        P("dp", "tensor"),
        P("dp", "tensor"),
        P("dp", "tensor"),
        P("tensor", None),
        P(None, "tensor"),
        P("tensor", None),
        P(None, "tensor"),
        P("tensor", "dp"),
        P("tensor", "dp"),
        P("dp", "tensor"),
        P(None, None, "tensor"),
    )
    return jax.shard_map(
        on_device, mesh=mesh, in_specs=placed, out_specs=P(None, None, "tensor"), check_vma=False
    )
```

time: 640 us -> 523 us (0.82)
  waiting for transfers between devices: 461 us -> 352 us
  matrix products: 138 us -> 106 us
  local copies, waits for them, and re-layouts: 1.63 us -> 31.1 us
  other arithmetic: 16.2 us -> 4.45 us
  starting transfers between devices: 1.02 us -> 10.3 us
    psum x4 -> x1, waiting for transfers between devices: 344 us -> 95.7 us  [on_device(): first_gradient = lax.psum(first_gradient, 'dp')]
    all_gather x2, waiting for transfers between devices: 47.4 us -> 95.6 us  [project(): out = lax.all_gather(out, 'dp', axis=0, tiled=True)]
    ppermute x0 -> x7, waiting for transfers between devices: none -> 43.6 us  [the longest x6 43.6 us: swap(): return lax.ppermute(value, 'tensor', ((0, 1), (1, 0)))]
    dot_general x16 -> x15, matrix products: 138 us -> 106 us  [the longest x14 105 us: dot(): lax.dot_general(left, right, (over, ((), ())), preferred_element_type=f32)]
    unnamed x10 -> x7, waiting for transfers between devices: 0.16 us -> 27.2 us
    reduce_scatter x4 -> x2, waiting for transfers between devices: 70.2 us -> 90 us  [project(): out = lax.psum_scatter(out, 'dp', scatter_dimension=0, tiled=True)]
    ppermute x0 -> x7, starting transfers between devices: none -> 9.85 us  [the longest x6 8.71 us: swap(): return lax.ppermute(value, 'tensor', ((0, 1), (1, 0)))]
    another operation x1 -> x0, other arithmetic: 7.76 us -> none  [on_device(): return jnp.stack(results)]
  transfers between devices with their start and end apart: 10 -> 13, of which waited for: 9 -> 8; matrix products, arithmetic and copies ran while one was open for 11% -> 16% of each run, Pallas kernels for 0% -> 0%
where the time goes in v1:
time: 523 us; the launch traced here: 518 us
  waiting for transfers between devices  352 us (67%)
  matrix products  106 us (20%)
  local copies, waits for them, and re-layouts  31.1 us (6%)
  between operations  14 us (3%)
  starting transfers between devices  10.3 us (2%)
    dot_general x14, matrix products, dot(): lax.dot_general(left, right, (over, ((), ())), preferred_element_type=f32)  105 us
    psum x1, waiting for transfers between devices, on_device(): first_gradient = lax.psum(first_gradient, 'dp')  95.7 us
    all_gather x2, waiting for transfers between devices, project(): out = lax.all_gather(out, 'dp', axis=0, tiled=True)  95.6 us
    reduce_scatter x2, waiting for transfers between devices, project(): out = lax.psum_scatter(out, 'dp', scatter_dimension=0, tiled=True)  90 us
    ppermute x6, waiting for transfers between devices, swap(): return lax.ppermute(value, 'tensor', ((0, 1), (1, 0)))  43.6 us
    unnamed x7, waiting for transfers between devices  27.2 us
  transfers between devices with their start and end apart: 13, of which 8 were waited for; matrix products, arithmetic and copies ran while one was open for 16% of the time, Pallas kernels for 0%

profile of v1, /device:TPU:0, one launch (start us, length us, event | category | flops | bytes accessed | tf_op | source)
XLA Modules:
  0.0 517.6 jit_solution(5538493977842545239)
XLA Ops:
  9.9 5.0 convolution_convert_fusion.4
  15.1 1.4 convolution_convert_fusion.5
  16.6 3.0 collective-permute-start
  19.6 3.5 collective-permute-done
  23.2 3.7 fusion
  26.8 3.7 fusion.1
  30.5 1.4 fusion.20
  32.0 4.2 pad_maximum_fusion
  36.2 6.1 %copy.14 = bf16[14784,128]{1,0:T(8,128)(2,1)} copy(bf16[14784,128]{0,1:T(8,128)(2,1)} %pad_maximum_fusion) | data formatting | bytes 7569408 | tf_op jit(solution)/shard_map/concatenate | solution.py:71
  42.3 4.2 pad.11
  49.3 13.8 %fusion.30 = bf16[2,256,1848]{1,2,0:T(8,128)(2,1)} fusion(bf16[4096,1848]{0,1:T(8,128)(2,1)} %param.18, bf16[2,512,4096]{2,1,0:T(8,128)(2,1)} %param.21, s32[]{:T(128)S(6)} %select_n.38), kind=kOutput, calls=%fused_computation.27 | convolution fusion | flops 7752019968 | bytes 21225476 | tf_op jit(solution)/shard_map/dot_general | solution.py:52
  63.1 1.7 collective-permute-start.1
  64.8 11.7 %fusion.40 = bf16[2,256,1848]{1,2,0:T(8,128)(2,1)} fusion(bf16[4096,1848]{0,1:T(8,128)(2,1)S(1)} %bitcast.78, bf16[2,512,4096]{2,1,0:T(8,128)(2,1)} %param.21, s32[]{:T(128)S(6)} %select_n.38), kind=kOutput, calls=%fused_computation.29 | convolution fusion | flops 7752019968 | bytes 21225476 | tf_op jit(solution)/shard_map/dot_general | solution.py:52
  76.9 13.6 %fusion.25 = bf16[2,256,1848]{1,2,0:T(8,128)(2,1)} fusion(bf16[4096,1848]{0,1:T(8,128)(2,1)} %param.18, bf16[2,512,4096]{2,1,0:T(8,128)(2,1)} %param.21, s32[]{:T(128)S(6)} %select_n.37), kind=kOutput, calls=%fused_computation.26 | convolution fusion | flops 7752019968 | bytes 21225476 | tf_op jit(solution)/shard_map/dot_general | solution.py:52
  90.6 27.1 %reduce-scatter.10.cloned.1.call-done = bf16[928,128]{1,0:T(8,128)(2,1)} async-done(((bf16[14848,128]{1,0:T(8,128)(2,1)}), bf16[928,128]{1,0:T(8,128)(2,1)}) %reduce-scatter.10.cloned.1.call-update) | async-done | bytes 237584
  120.0 95.7 %all-reduce.5.cloned.1.call-done = bf16[4096,128]{0,1:T(8,128)(2,1)} async-done(((bf16[4096,128]{0,1:T(8,128)(2,1)}), bf16[4096,128]{0,1:T(8,128)(2,1)}) %all-reduce.5.cloned.1.call-update) | async-done | bytes 1048592 | tf_op jit(solution)/shard_map/psum | solution.py:88
  215.7 6.5 %fusion.47 = f32[2,512,128]{1,2,0:T(8,128)S(1)} fusion(bf16[2,512,4096]{2,1,0:T(8,128)(2,1)} %param.21, bf16[4096,128]{0,1:T(8,128)(2,1)} %all-reduce.5.cloned.1.call-done, bf16[4096,128]{0,1:T(8,128)(2,1)S(1)} %constant_dynamic-update-slice_fusion), kind=kOutput, calls=%fused_computation.38 | convolution fusion | flops 1076363264 | bytes 11010048 | tf_op jit(solution)/shard_map/dot_general | solution.py:52
  222.2 1.5 collective-permute-start.2
  224.3 12.6 %fusion.35 = bf16[2,256,1848]{1,2,0:T(8,128)(2,1)S(1)} fusion(bf16[4096,1848]{0,1:T(8,128)(2,1)} %param.19, bf16[2,512,4096]{2,1,0:T(8,128)(2,1)} %param.21, s32[]{:T(128)S(6)} %select_n.37), kind=kOutput, calls=%fused_computation.28 | convolution fusion | flops 7752019968 | bytes 21225476 | tf_op jit(solution)/shard_map/dot_general | solution.py:52
  238.5 4.8 multiply_convert_fusion
  244.2 11.3 %fusion.14 = bf16[2,256,4096]{2,1,0:T(8,128)(2,1)} fusion(bf16[2,256,1848]{1,2,0:T(8,128)(2,1)S(1)} %multiply_convert_fusion, bf16[1848,4096]{1,0:T(8,128)(2,1)S(1)} %bitcast.80), kind=kOutput, calls=%fused_computation.16 | convolution fusion | flops 7753170944 | bytes 21225472 | tf_op jit(solution)/shard_map/dot_general | solution.py:52
  255.6 1.4 copy-done.7
  257.1 1.6 collective-permute-start.6
  258.6 40.0 %collective-permute-done.6 = bf16[2,256,1848]{1,2,0:T(8,128)(2,1)S(1)} collective-permute-done((bf16[2,256,1848]{1,2,0:T(8,128)(2,1)S(1)}, bf16[2,256,1848]{1,2,0:T(8,128)(2,1)S(1)}, u32[]{:S(2)}, u32[]{:S(2)}) %collective-permute-start.6) | collective-permute-done | bytes 1892384 | tf_op jit(solution)/shard_map/ppermute | solution.py:14
  298.7 14.5 %fusion.17 = bf16[2,256,4096]{2,1,0:T(8,128)(2,1)} fusion(bf16[2,256,1848]{1,2,0:T(8,128)(2,1)S(1)} %collective-permute-done.6, bf16[1848,4096]{1,0:T(8,128)(2,1)} %param.20), kind=kOutput, calls=%fused_computation.17 | convolution fusion | flops 7753170944 | bytes 21225472 | tf_op jit(solution)/shard_map/dot_general | solution.py:52
  313.2 14.5 %reduce-scatter.6.cloned.1.call-done = bf16[32,4096]{1,0:T(8,128)(2,1)} async-done(((bf16[512,4096]{1,0:T(8,128)(2,1)}), bf16[32,4096]{1,0:T(8,128)(2,1)}) %reduce-scatter.6.cloned.1.call-update) | async-done | bytes 262160 | tf_op jit(solution)/shard_map/reduce_scatter | solution.py:160
  327.7 75.6 %reduce-scatter.8.cloned.1.call-done = bf16[32,4096]{1,0:T(8,128)(2,1)} async-done(((bf16[512,4096]{1,0:T(8,128)(2,1)}), bf16[32,4096]{1,0:T(8,128)(2,1)}) %reduce-scatter.8.cloned.1.call-update) | async-done | bytes 262160 | tf_op jit(solution)/shard_map/reduce_scatter | solution.py:160
  403.3 51.4 %all-gather.3.cloned.1.call-done = bf16[512,4096]{1,0:T(8,128)(2,1)} async-done(((bf16[32,4096]{1,0:T(8,128)(2,1)}), bf16[512,4096]{1,0:T(8,128)(2,1)}) %all-gather.3.cloned.1.call-update) | async-done | bytes 4194320 | tf_op jit(solution)/shard_map/all_gather | solution.py:161
  454.7 4.4 broadcast_in_dim.3
  459.2 2.3 constant_dynamic-update-slice_fusion.3
  461.5 44.2 %all-gather.5.cloned.1.call-done = bf16[512,4096]{1,0:T(8,128)(2,1)} async-done(((bf16[32,4096]{1,0:T(8,128)(2,1)}), bf16[512,4096]{1,0:T(8,128)(2,1)}) %all-gather.5.cloned.1.call-update) | async-done | bytes 4194320 | tf_op jit(solution)/shard_map/all_gather | solution.py:161
  505.7 4.8 constant_dynamic-update-slice_fusion.2
  (77 shorter events, 12.1 us)
Async XLA Ops:
  6.5 2.4 copy-start
  6.5 111.2 %reduce-scatter.10.cloned.1.call-start = ((), (), s32[]{:S(2)}) async-start(), calls=%async_computation.8 | async-start | bytes 4038656
  6.5 3.3 copy-start.2
  9.0 5.9 %slice-start = ((s8[7569408]{0:T(1024)(128)(4,1)}), s8[4194304]{0:T(1024)(128)(4,1)S(1)}, s32[]{:S(2)}) async-start(s8[7569408]{0:T(1024)(128)(4,1)} %bitcast.67), calls=%async_computation.9 | async-start | bytes 8388608
  9.8 5.0 slice-start.1
  9.9 5.3 %copy-start.4 = (bf16[64,14784]{1,0:T(8,128)(2,1)S(1)}, bf16[64,14784]{1,0:T(8,128)(2,1)}, u32[]{:S(2)}) copy-start(bf16[64,14784]{1,0:T(8,128)(2,1)} %param.15) | copy-start | bytes 5677060
  16.5 10.3 %slice-start.2 = ((s8[7569408]{0:T(1024)(128)(4,1)}), s8[4194304]{0:T(1024)(128)(4,1)S(1)}, s32[]{:S(2)}) async-start(s8[7569408]{0:T(1024)(128)(4,1)} %bitcast.69), calls=%async_computation.11 | async-start | bytes 8388608
  16.6 6.5 %collective-permute-start = (bf16[256,256]{0,1:T(8,128)(2,1)S(1)}, bf16[256,256]{0,1:T(8,128)(2,1)S(1)}, u32[]{:S(2)}, u32[]{:S(2)}) collective-permute-start(bf16[256,256]{0,1:T(8,128)(2,1)S(1)} %pad_maximum_fusion.2), channel_id=1, source_target_pairs={{0,1},{1,0},{2,3},{3,2},{4,5},{5,4},{6,7},{7,6},{8,9},{9,8},{10,11... | collective-permute-start | bytes 393224 | tf_op jit(solution)/shard_map/ppermute | solution.py:14
  23.1 3.7 slice-start.3
  46.5 1.5 copy-start.3
  46.5 169.2 %all-reduce.5.cloned.1.call-start = ((), (), s32[]{:S(2)}) async-start(), calls=%async_computation.3 | async-start | bytes 2097152 | tf_op jit(solution)/shard_map/psum | solution.py:88
  48.0 16.8 %slice-start.4 = ((s8[15138816]{0:T(1024)(128)(4,1)}), s8[4194304]{0:T(1024)(128)(4,1)S(1)}, s32[]{:S(2)}) async-start(s8[15138816]{0:T(1024)(128)(4,1)} %bitcast.77), calls=%async_computation.13 | async-start | bytes 8388608
  49.2 15.5 %slice-start.5 = ((s8[15138816]{0:T(1024)(128)(4,1)}), s8[4194304]{0:T(1024)(128)(4,1)S(1)}, s32[]{:S(2)}) async-start(s8[15138816]{0:T(1024)(128)(4,1)} %bitcast.77), calls=%async_computation.14 | async-start | bytes 8388608
  49.2 15.5 %slice-start.6 = ((s8[15138816]{0:T(1024)(128)(4,1)}), s8[4194304]{0:T(1024)(128)(4,1)S(1)}, s32[]{:S(2)}) async-start(s8[15138816]{0:T(1024)(128)(4,1)} %bitcast.77), calls=%async_computation.15 | async-start | bytes 8388608
  49.3 15.5 %slice-start.7 = ((s8[15138816]{0:T(1024)(128)(4,1)}), s8[2555904]{0:T(1024)(128)(4,1)S(1)}, s32[]{:S(2)}) async-start(s8[15138816]{0:T(1024)(128)(4,1)} %bitcast.77), calls=%async_computation.16 | async-start | bytes 5111808
  63.1 174.8 %collective-permute-start.1 = (bf16[2,256,1848]{1,2,0:T(8,128)(2,1)}, bf16[2,256,1848]{1,2,0:T(8,128)(2,1)}, u32[]{:S(2)}, u32[]{:S(2)}) collective-permute-start(bf16[2,256,1848]{1,2,0:T(8,128)(2,1)} %fusion.30), channel_id=1, source_target_pairs={{0,1},{1,0},{2,3},{3,2},{4,5},{5,4},{6,7},{7,6},{8,9},{9,8},{10,11... | collective-permute-start | bytes 5677064 | tf_op jit(solution)/shard_map/ppermute | solution.py:14
  76.5 161.4 %collective-permute-start.5 = (bf16[2,256,1848]{1,2,0:T(8,128)(2,1)}, bf16[2,256,1848]{1,2,0:T(8,128)(2,1)}, u32[]{:S(2)}, u32[]{:S(2)}) collective-permute-start(bf16[2,256,1848]{1,2,0:T(8,128)(2,1)} %fusion.40), channel_id=1, source_target_pairs={{0,1},{1,0},{2,3},{3,2},{4,5},{5,4},{6,7},{7,6},{8,9},{9,8},{10,11... | collective-permute-start | bytes 5677064 | tf_op jit(solution)/shard_map/ppermute | solution.py:14
  76.9 250.8 %reduce-scatter.6.cloned.1.call-start = ((), (), s32[]{:S(2)}) async-start(), calls=%async_computation.4 | async-start | bytes 4456448 | tf_op jit(solution)/shard_map/reduce_scatter | solution.py:160
  118.9 104.9 %collective-permute-start.3 = (bf16[928,128]{0,1:T(8,128)(2,1)S(1)}, bf16[928,128]{0,1:T(8,128)(2,1)S(1)}, u32[]{:S(2)}, u32[]{:S(2)}) collective-permute-start(bf16[928,128]{0,1:T(8,128)(2,1)S(1)} %subtract_convert_fusion.1), channel_id=1, source_target_pairs={{0,0},{1,16},{2,1},{3,17},{4,2},{5,18},{6,3},{7,19},{8,4},{9,20},{... | collective-permute-start | bytes 712712 | tf_op jit(solution)/shard_map/ppermute | solution.py:129
  222.2 14.7 %collective-permute-start.2 = (bf16[2,256,128]{1,2,0:T(8,128)(2,1)S(1)}, bf16[2,256,128]{1,2,0:T(8,128)(2,1)S(1)}, u32[]{:S(2)}, u32[]{:S(2)}) collective-permute-start(bf16[2,256,128]{1,2,0:T(8,128)(2,1)S(1)} %dynamic-slice_convert_fusion), channel_id=1, source_target_pairs={{0,1},{1,0},{2,3},{3,2},{4,5},{5,4},{6,7},{7,6},{8,9},{9,8},{10,11... | collective-permute-start | bytes 393224 | tf_op jit(solution)/shard_map/ppermute | solution.py:14
  223.8 13.3 %collective-permute-start.4 = (bf16[928,128]{0,1:T(8,128)(2,1)S(1)}, bf16[928,128]{0,1:T(8,128)(2,1)S(1)}, u32[]{:S(2)}, u32[]{:S(2)}) collective-permute-start(bf16[928,128]{0,1:T(8,128)(2,1)S(1)} %collective-permute-done.3), channel_id=1, source_target_pairs={{0,1},{1,0},{2,3},{3,2},{4,5},{5,4},{6,7},{7,6},{8,9},{9,8},{10,11... | collective-permute-start | bytes 712712 | tf_op jit(solution)/shard_map/ppermute | solution.py:14
  237.1 6.2 %slice-start.8 = ((s8[15138816]{0:T(1024)(128)(4,1)}), s8[4194304]{0:T(1024)(128)(4,1)S(1)}, s32[]{:S(2)}) async-start(s8[15138816]{0:T(1024)(128)(4,1)} %bitcast.79), calls=%async_computation.17 | async-start | bytes 8388608
  237.8 5.5 %slice-start.9 = ((s8[15138816]{0:T(1024)(128)(4,1)}), s8[4194304]{0:T(1024)(128)(4,1)S(1)}, s32[]{:S(2)}) async-start(s8[15138816]{0:T(1024)(128)(4,1)} %bitcast.79), calls=%async_computation.18 | async-start | bytes 8388608
  237.8 5.7 %slice-start.10 = ((s8[15138816]{0:T(1024)(128)(4,1)}), s8[4194304]{0:T(1024)(128)(4,1)S(1)}, s32[]{:S(2)}) async-start(s8[15138816]{0:T(1024)(128)(4,1)} %bitcast.79), calls=%async_computation.19 | async-start | bytes 8388608
  237.8 6.4 %slice-start.11 = ((s8[15138816]{0:T(1024)(128)(4,1)}), s8[2555904]{0:T(1024)(128)(4,1)S(1)}, s32[]{:S(2)}) async-start(s8[15138816]{0:T(1024)(128)(4,1)} %bitcast.79), calls=%async_computation.20 | async-start | bytes 5111808
  244.2 11.3 %copy-start.6 = (bf16[2,256,1848]{1,2,0:T(8,128)(2,1)}, bf16[2,256,1848]{1,2,0:T(8,128)(2,1)S(1)}, u32[]{:S(2)}) copy-start(bf16[2,256,1848]{1,2,0:T(8,128)(2,1)S(1)} %multiply_convert_fusion) | copy-start | bytes 5677060
  255.6 147.7 %reduce-scatter.8.cloned.1.call-start = ((), (), s32[]{:S(2)}) async-start(), calls=%async_computation.6 | async-start | bytes 4456448 | tf_op jit(solution)/shard_map/reduce_scatter | solution.py:160
  257.1 41.6 %collective-permute-start.6 = (bf16[2,256,1848]{1,2,0:T(8,128)(2,1)S(1)}, bf16[2,256,1848]{1,2,0:T(8,128)(2,1)S(1)}, u32[]{:S(2)}, u32[]{:S(2)}) collective-permute-start(bf16[2,256,1848]{1,2,0:T(8,128)(2,1)S(1)} %copy-done.7), channel_id=1, source_target_pairs={{0,1},{1,0},{2,3},{3,2},{4,5},{5,4},{6,7},{7,6},{8,9},{9,8},{10,11... | collective-permute-start | bytes 5677064 | tf_op jit(solution)/shard_map/ppermute | solution.py:14
  313.2 141.6 %all-gather.3.cloned.1.call-start = ((), (), s32[]{:S(2)}) async-start(), calls=%async_computation.5 | async-start | bytes 4456448 | tf_op jit(solution)/shard_map/all_gather | solution.py:161
  327.7 178.0 %all-gather.5.cloned.1.call-start = ((), (), s32[]{:S(2)}) async-start(), calls=%async_computation.7 | async-start | bytes 4456448 | tf_op jit(solution)/shard_map/all_gather | solution.py:161
  454.7 4.4 copy-start.5
  505.7 4.9 copy-start.1
  (2 other events, 3.0 us)
Sparse Core Ops, SparseCore 0:
  46.6 71.0 reduce-scatter.9
  121.2 94.4 all-reduce.4
  255.7 71.9 reduce-scatter.5
  331.4 71.8 reduce-scatter.7
  405.3 49.3 all-gather.2
  456.8 48.8 all-gather.4
